TPU v7x, 32 devices: a whole 2x2x4 slice. The times are simulated.
32 devices in a mesh: rows: 8 (over z, x), leaf: 4 (over y, core).
Axes of the slice: x: 2, y: 2, z: 4, core: 2. Of those that a mesh axis runs over, the one named last changes fastest.
Arguments:
- right_sides: float32 [65536, 128], P(('rows', 'leaf')), may hold values from -30 to 30
- near_blocks: bfloat16 [2, 128, 512, 512], P(None, ('rows', 'leaf')), may hold values from -1 to 2.4
- leaf_bases: bfloat16 [2, 128, 2, 512, 128], P(None, ('rows', 'leaf')), may hold values from -1.5 to 1.5
- local_factors: bfloat16 [2, 224, 3, 128, 128], P(None, ('rows', 'leaf')), may hold values from -1.7 to 1.7
- upper_factors: bfloat16 [2, 32, 3, 3, 128, 128], P(None, ('rows', 'leaf')), may hold values from -1.7 to 1.7, as said below
- top_couplings: bfloat16 [2, 2, 128, 128], replicated, may hold values from -0.5 to 0.5
Outputs:
- solution: float32 [65536, 128], P(('rows', 'leaf'))
- residual_norms: float32 [3, 128], replicated
Inputs may be any that keep to these rules, and one draw needn't show every extreme that they name: upper_factors[s, d, h] is the same for all devices d with the same d // 2 ** (h + 1): the factors of the node h + 1 levels above device d's own node.
All inputs are finite; a program needn't handle non-finite values.
Results may differ from a plain program's by a relative error of at most 0.00095.
Values sent between devices are 32-bit elements; how exact they have to be, the bound alone decides.
A program may use at most 128 MiB of HBM per device.

v0:
```python
import jax
import jax.numpy as jnp
from jax import lax
from jax.sharding import PartitionSpec as P

STEPS = 3


HIGHEST = lax.Precision.HIGHEST


def swapped(value, axis, distance):
    mask = 2**distance
    pairs = [(source, source ^ mask) for source in range(lax.axis_size(axis))]
    return lax.ppermute(value, axis, pairs)


def split_pair(values):
    upper_half = lax.optimization_barrier(values.astype(jnp.bfloat16))
    lower_half = (values - upper_half.astype(jnp.float32)).astype(jnp.bfloat16)
    return (upper_half, lower_half)


def sibling_of(values):
    shaped = values.reshape((values.shape[0] // 2, 2) + values.shape[1:])
    return shaped[:, ::-1].reshape(values.shape)


def parity(position, shift):
    return position // 2**shift % 2


def apply_device(operand_set, pieces, split_far, positions):
    near_set, basis_set, local_set, upper_set, top_set = operand_set
    leaf_position, row_position, bits_leaf, bits_rows = positions
    near_field = None
    coefficient = None
    for piece_value in pieces:
        near_term = jnp.einsum(
            "lij,ljc->lic", near_set, piece_value, preferred_element_type=jnp.float32
        )
        coefficient_term = jnp.einsum(
            "lir,lic->lrc", basis_set[:, 1], piece_value, preferred_element_type=jnp.float32
        )
        if near_field is None:
            near_field = near_term
            coefficient = coefficient_term
        else:
            near_field = near_field + near_term
            coefficient = coefficient + coefficient_term
    factors = local_set.astype(jnp.float32)
    lower_list = []
    table_list = []
    offset = 0
    node_count = near_set.shape[0]
    while node_count > 1:
        factor_table = factors[offset : offset + node_count]
        lower_list.append(coefficient)
        table_list.append(factor_table)
        projected = jnp.einsum("nab,nac->nbc", factor_table[:, 0], coefficient, precision=HIGHEST)
        coefficient = projected[0::2] + projected[1::2]
        offset = offset + node_count
        node_count = node_count // 2
    coefficient = coefficient[0]
    cross_tables = [factors[offset]] + [
        upper_set[upper_index] for upper_index in range(upper_set.shape[0])
    ]
    levels_up = bits_leaf + bits_rows
    sibling_list = []
    for height in range(bits_leaf):
        projected = jnp.dot(cross_tables[height][0].T, coefficient, precision=HIGHEST)
        sibling, sibling_projected = swapped((coefficient, projected), "leaf", height)
        sibling_list.append(sibling)
        coefficient = projected + sibling_projected
    for height in range(bits_leaf, levels_up):
        if height == levels_up - 1:
            sibling_list.append(swapped(coefficient, "rows", bits_rows - 1))
        else:
            projected = jnp.dot(cross_tables[height][0].T, coefficient, precision=HIGHEST)
            sibling, sibling_projected = swapped(
                (coefficient, projected), "rows", height - bits_leaf
            )
            sibling_list.append(sibling)
            coefficient = projected + sibling_projected
    top_position = parity(row_position, bits_rows - 1)
    top_block = lax.dynamic_index_in_dim(top_set, top_position, 0, keepdims=False).astype(
        jnp.float32
    )
    far_field = jnp.dot(top_block, sibling_list[levels_up - 1], precision=HIGHEST)
    for height in range(levels_up - 2, -1, -1):
        factor_table = cross_tables[height]
        far_field = jnp.dot(factor_table[1], far_field, precision=HIGHEST) + jnp.dot(
            factor_table[2], sibling_list[height], precision=HIGHEST
        )
    far_field = far_field[None]
    for factor_table, lower_value in zip(table_list[::-1], lower_list[::-1]):
        far_field = jnp.einsum(
            "nab,nbc->nac", factor_table[:, 1], jnp.repeat(far_field, 2, axis=0), precision=HIGHEST
        ) + jnp.einsum(
            "nab,nbc->nac", factor_table[:, 2], sibling_of(lower_value), precision=HIGHEST
        )
    if split_far:
        far_parts = split_pair(far_field)
    else:
        far_parts = (far_field.astype(jnp.bfloat16),)
    output = near_field
    for piece_value in far_parts:
        output = output + jnp.einsum(
            "lir,lrc->lic", basis_set[:, 0], piece_value, preferred_element_type=jnp.float32
        )
    return output


def body(right_sides, near_blocks, leaf_bases, local_factors, upper_factors, top_couplings):
    bits_leaf = lax.axis_size("leaf").bit_length() - 1
    bits_rows = lax.axis_size("rows").bit_length() - 1
    positions = (lax.axis_index("leaf"), lax.axis_index("rows"), bits_leaf, bits_rows)
    leaf_count = near_blocks.shape[1]
    column_count = right_sides.shape[1]
    right_side = right_sides.reshape(leaf_count, -1, column_count)
    operand_sets = []
    for member in range(2):
        operand_sets.append(
            (
                near_blocks[member],
                leaf_bases[member],
                local_factors[member],
                upper_factors[member, 0].astype(jnp.float32),
                top_couplings[member],
            )
        )
    solution = apply_device(operand_sets[1], (right_side.astype(jnp.bfloat16),), False, positions)
    norm_list = []
    for refine_step in range(STEPS):
        residual = right_side - apply_device(operand_sets[0], split_pair(solution), True, positions)
        partial_norm = jnp.sum(residual * residual, axis=(0, 1))
        norm_list.append(lax.psum(partial_norm, ("rows", "leaf")))
        solution = solution + apply_device(
            operand_sets[1], (residual.astype(jnp.bfloat16),), False, positions
        )
    norm_table = jnp.stack(norm_list)
    return (solution.reshape(-1, column_count), norm_table)


def solution(mesh):
    placed = (
        P(("rows", "leaf"), None),
        P(None, ("rows", "leaf"), None, None),
        P(None, ("rows", "leaf"), None, None, None),
        P(None, ("rows", "leaf"), None, None, None),
        P(None, ("rows", "leaf"), None, None, None, None),
        P(),
    )
    return jax.shard_map(
        body,
        mesh=mesh,
        in_specs=placed,
        out_specs=(P(("rows", "leaf"), None), P()),
        check_vma=False,
    )
```

profile of v0, /device:TPU:0, one launch (start us, length us, event | category | flops | bytes accessed | tf_op | source)
XLA Modules:
  0.0 351.0 jit_solution(10490166994885296596)
XLA Ops:
  0.6 1.9 fusion.341
  2.6 2.1 fusion.342
  6.4 2.0 copy_bitcast_fusion.1
  14.0 2.9 collective-permute-start.1
  16.9 2.4 collective-permute-done.1
  20.2 1.9 collective-permute-start.2
  22.1 2.4 collective-permute-done.2
  25.3 2.0 collective-permute-start.3
  27.3 1.7 fusion.18
  30.3 2.9 collective-permute-start.4
  60.6 3.8 %collective-permute-done.10 = f32[128,128]{0,1:T(8,128)S(1)} collective-permute-done((f32[128,128]{0,1:T(8,128)S(1)}, f32[128,128]{0,1:T(8,128)S(1)}, u32[]{:S(2)}, u32[]{:S(2)}) %collective-permute-start.10) | collective-permute-done | bytes 65568 | tf_op jit(solution)/shard_map/ppermute | solution.py:15
  67.1 2.5 copy.61
  74.7 2.6 fusion.8
  78.4 1.8 fusion.33
  105.9 2.7 collective-permute-done.19
  111.2 2.7 collective-permute-done.20
  114.9 1.7 collective-permute-start.21
  116.6 2.6 collective-permute-done.21
  119.9 2.7 collective-permute-start.22
  122.6 1.9 fusion.16
  130.8 1.8 collective-permute-start.23
  154.4 3.8 %collective-permute-done.28 = f32[128,128]{0,1:T(8,128)S(1)} collective-permute-done((f32[128,128]{0,1:T(8,128)S(1)}, f32[128,128]{0,1:T(8,128)S(1)}, u32[]{:S(2)}, u32[]{:S(2)}) %collective-permute-start.28) | collective-permute-done | bytes 65568 | tf_op jit(solution)/shard_map/ppermute | solution.py:15
  159.0 3.7 %collective-permute-done.29 = f32[128,128]{0,1:T(8,128)S(1)} collective-permute-done((f32[128,128]{0,1:T(8,128)S(1)}, f32[128,128]{0,1:T(8,128)S(1)}, u32[]{:S(2)}, u32[]{:S(2)}) %collective-permute-start.29) | collective-permute-done | bytes 65568 | tf_op jit(solution)/shard_map/ppermute | solution.py:15
  163.3 1.8 collective-permute-start.30
  168.6 1.8 fusion.36
  172.0 1.7 rev.31
  192.4 2.7 collective-permute-done.37
  197.7 2.7 collective-permute-done.38
  201.3 1.7 collective-permute-start.39
  203.1 2.6 collective-permute-done.39
  206.3 2.7 collective-permute-start.40
  209.0 1.7 fusion.14
  217.0 1.9 collective-permute-start.41
  234.0 1.8 fusion.348
  243.0 3.7 %collective-permute-done.46 = f32[128,128]{0,1:T(8,128)S(1)} collective-permute-done((f32[128,128]{0,1:T(8,128)S(1)}, f32[128,128]{0,1:T(8,128)S(1)}, u32[]{:S(2)}, u32[]{:S(2)}) %collective-permute-start.46) | collective-permute-done | bytes 65568 | tf_op jit(solution)/shard_map/ppermute | solution.py:15
  248.4 3.7 %collective-permute-done.47 = f32[128,128]{0,1:T(8,128)S(1)} collective-permute-done((f32[128,128]{0,1:T(8,128)S(1)}, f32[128,128]{0,1:T(8,128)S(1)}, u32[]{:S(2)}, u32[]{:S(2)}) %collective-permute-start.47) | collective-permute-done | bytes 65568 | tf_op jit(solution)/shard_map/ppermute | solution.py:15
  253.1 2.0 collective-permute-start.48
  258.5 1.8 fusion.39
  264.5 1.7 collective-permute-start.50
  283.6 2.7 collective-permute-done.55
  288.1 2.7 collective-permute-done.56
  291.0 1.7 collective-permute-start.57
  292.7 1.7 fusion.12
  294.4 40.9 %all-reduce = (f32[1,128]{1,0:T(1,128)S(1)}, f32[1,128]{1,0:T(1,128)S(1)}, f32[1,128]{1,0:T(1,128)S(1)}) all-reduce(f32[1,128]{1,0:T(1,128)S(1)} %bitcast.750, f32[1,128]{1,0:T(1,128)S(1)} %bitcast.749, f32[1,128]{1,0:T(1,128)S(1)} %bitcast.748), channel_id=1, replica_groups=mesh['rows'=8,'leaf'=4] {'rows','leaf'}, use_global_device_ids=true, to_apply=%region_5.6 | all-reduce | flops 384 | bytes 3072 | tf_op jit(solution)/shard_map/psum | solution.py:137
  336.8 2.3 collective-permute-start.61
  339.6 2.0 collective-permute-start.59
  342.1 1.8 collective-permute-done.59
  348.4 2.5 fusion.21
  (485 shorter events, 196.9 us)
Async XLA Ops:
  14.0 5.3 %collective-permute-start.1 = (f32[128,128]{0,1:T(8,128)S(1)}, f32[128,128]{0,1:T(8,128)S(1)}, u32[]{:S(2)}, u32[]{:S(2)}) collective-permute-start(f32[128,128]{0,1:T(8,128)S(1)} %convolution_bitcast_fusion.41), channel_id=1, source_target_pairs={{0,2},{1,3},{2,0},{3,1},{4,6},{5,7},{6,4},{7,5},{8,10},{9,11},{10,... | collective-permute-start | bytes 196616 | tf_op jit(solution)/shard_map/ppermute | solution.py:15
  20.2 4.3 %collective-permute-start.2 = (f32[128,128]{0,1:T(8,128)S(1)}, f32[128,128]{0,1:T(8,128)S(1)}, u32[]{:S(2)}, u32[]{:S(2)}) collective-permute-start(f32[128,128]{0,1:T(8,128)S(1)} %convolution_bitcast_fusion.40), channel_id=1, source_target_pairs={{0,4},{4,0},{8,12},{12,8},{16,20},{20,16},{24,28},{28,24},{1,5},{5... | collective-permute-start | bytes 196616 | tf_op jit(solution)/shard_map/ppermute | solution.py:15
  22.0 25.0 %collective-permute-start.8 = (f32[128,128]{0,1:T(8,128)}, f32[128,128]{0,1:T(8,128)}, u32[]{:S(2)}, u32[]{:S(2)}) collective-permute-start(f32[128,128]{0,1:T(8,128)} %fusion.101), channel_id=1, source_target_pairs={{0,1},{1,0},{2,3},{3,2},{4,5},{5,4},{6,7},{7,6},{8,9},{9,8},{10,11... | collective-permute-start | bytes 196616 | tf_op jit(solution)/shard_map/ppermute | solution.py:15
  25.3 4.3 %collective-permute-start.3 = (f32[128,128]{0,1:T(8,128)S(1)}, f32[128,128]{0,1:T(8,128)S(1)}, u32[]{:S(2)}, u32[]{:S(2)}) collective-permute-start(f32[128,128]{0,1:T(8,128)S(1)} %convolution_bitcast_fusion.39), channel_id=1, source_target_pairs={{0,8},{4,12},{8,0},{12,4},{16,24},{20,28},{24,16},{28,20},{1,9},{5... | collective-permute-start | bytes 196616 | tf_op jit(solution)/shard_map/ppermute | solution.py:15
  30.3 11.8 %collective-permute-start.4 = (f32[128,128]{0,1:T(8,128)}, f32[128,128]{0,1:T(8,128)}, u32[]{:S(2)}, u32[]{:S(2)}) collective-permute-start(f32[128,128]{0,1:T(8,128)} %add.452), channel_id=1, source_target_pairs={{0,16},{4,20},{8,24},{12,28},{16,0},{20,4},{24,8},{28,12},{1,17},{... | collective-permute-start | bytes 196616 | tf_op jit(solution)/shard_map/ppermute | solution.py:15
  37.5 8.4 %collective-permute-start.7 = (f32[128,128]{0,1:T(8,128)}, f32[128,128]{0,1:T(8,128)S(1)}, u32[]{:S(2)}, u32[]{:S(2)}) collective-permute-start(f32[128,128]{0,1:T(8,128)} %copy-done.59), channel_id=1, source_target_pairs={{0,2},{1,3},{2,0},{3,1},{4,6},{5,7},{6,4},{7,5},{8,10},{9,11},{10,... | collective-permute-start | bytes 196616 | tf_op jit(solution)/shard_map/ppermute | solution.py:15
  39.0 6.4 %collective-permute-start.6 = (f32[128,128]{0,1:T(8,128)}, f32[128,128]{0,1:T(8,128)S(1)}, u32[]{:S(2)}, u32[]{:S(2)}) collective-permute-start(f32[128,128]{0,1:T(8,128)} %copy-done.60), channel_id=1, source_target_pairs={{0,4},{4,0},{8,12},{12,8},{16,20},{20,16},{24,28},{28,24},{1,5},{5... | collective-permute-start | bytes 196616 | tf_op jit(solution)/shard_map/ppermute | solution.py:15
  40.5 4.5 %collective-permute-start.5 = (f32[128,128]{0,1:T(8,128)}, f32[128,128]{0,1:T(8,128)S(1)}, u32[]{:S(2)}, u32[]{:S(2)}) collective-permute-start(f32[128,128]{0,1:T(8,128)} %copy-done.61), channel_id=1, source_target_pairs={{0,8},{4,12},{8,0},{12,4},{16,24},{20,28},{24,16},{28,20},{1,9},{5... | collective-permute-start | bytes 196616 | tf_op jit(solution)/shard_map/ppermute | solution.py:15
  60.1 4.3 %collective-permute-start.10 = (f32[128,128]{0,1:T(8,128)S(1)}, f32[128,128]{0,1:T(8,128)S(1)}, u32[]{:S(2)}, u32[]{:S(2)}) collective-permute-start(f32[128,128]{0,1:T(8,128)S(1)} %convolution_bitcast_fusion.37), channel_id=1, source_target_pairs={{0,2},{1,3},{2,0},{3,1},{4,6},{5,7},{6,4},{7,5},{8,10},{9,11},{10,... | collective-permute-start | bytes 196616 | tf_op jit(solution)/shard_map/ppermute | solution.py:15
  66.6 4.6 %collective-permute-start.11 = (f32[128,128]{0,1:T(8,128)}, f32[128,128]{0,1:T(8,128)}, u32[]{:S(2)}, u32[]{:S(2)}) collective-permute-start(f32[128,128]{0,1:T(8,128)} %convolution_bitcast_fusion.36), channel_id=1, source_target_pairs={{0,4},{4,0},{8,12},{12,8},{16,20},{20,16},{24,28},{28,24},{1,5},{5... | collective-permute-start | bytes 196616 | tf_op jit(solution)/shard_map/ppermute | solution.py:15
  73.1 4.3 %collective-permute-start.12 = (f32[128,128]{0,1:T(8,128)S(1)}, f32[128,128]{0,1:T(8,128)S(1)}, u32[]{:S(2)}, u32[]{:S(2)}) collective-permute-start(f32[128,128]{0,1:T(8,128)S(1)} %convolution_bitcast_fusion.35), channel_id=1, source_target_pairs={{0,8},{4,12},{8,0},{12,4},{16,24},{20,28},{24,16},{28,20},{1,9},{5... | collective-permute-start | bytes 196616 | tf_op jit(solution)/shard_map/ppermute | solution.py:15
  78.0 8.0 %collective-permute-start.13 = (f32[128,128]{0,1:T(8,128)}, f32[128,128]{0,1:T(8,128)}, u32[]{:S(2)}, u32[]{:S(2)}) collective-permute-start(f32[128,128]{0,1:T(8,128)} %add.469), channel_id=1, source_target_pairs={{0,16},{4,20},{8,24},{12,28},{16,0},{20,4},{24,8},{28,12},{1,17},{... | collective-permute-start | bytes 196616 | tf_op jit(solution)/shard_map/ppermute | solution.py:15
  81.7 13.0 %collective-permute-start.17 = (f32[128,128]{0,1:T(8,128)}, f32[128,128]{0,1:T(8,128)}, u32[]{:S(2)}, u32[]{:S(2)}) collective-permute-start(f32[128,128]{0,1:T(8,128)} %copy-done.62), channel_id=1, source_target_pairs={{0,1},{1,0},{2,3},{3,2},{4,5},{5,4},{6,7},{7,6},{8,9},{9,8},{10,11... | collective-permute-start | bytes 196616 | tf_op jit(solution)/shard_map/ppermute | solution.py:15
  83.4 9.4 %collective-permute-start.16 = (f32[128,128]{0,1:T(8,128)}, f32[128,128]{0,1:T(8,128)S(1)}, u32[]{:S(2)}, u32[]{:S(2)}) collective-permute-start(f32[128,128]{0,1:T(8,128)} %copy-done.67), channel_id=1, source_target_pairs={{0,2},{1,3},{2,0},{3,1},{4,6},{5,7},{6,4},{7,5},{8,10},{9,11},{10,... | collective-permute-start | bytes 196616 | tf_op jit(solution)/shard_map/ppermute | solution.py:15
  83.9 6.9 %collective-permute-start.15 = (f32[128,128]{0,1:T(8,128)}, f32[128,128]{0,1:T(8,128)S(1)}, u32[]{:S(2)}, u32[]{:S(2)}) collective-permute-start(f32[128,128]{0,1:T(8,128)} %copy-done.72), channel_id=1, source_target_pairs={{0,4},{4,0},{8,12},{12,8},{16,20},{20,16},{24,28},{28,24},{1,5},{5... | collective-permute-start | bytes 196616 | tf_op jit(solution)/shard_map/ppermute | solution.py:15
  84.4 4.5 %collective-permute-start.14 = (f32[128,128]{0,1:T(8,128)}, f32[128,128]{0,1:T(8,128)S(1)}, u32[]{:S(2)}, u32[]{:S(2)}) collective-permute-start(f32[128,128]{0,1:T(8,128)} %copy-done.77), channel_id=1, source_target_pairs={{0,8},{4,12},{8,0},{12,4},{16,24},{20,28},{24,16},{28,20},{1,9},{5... | collective-permute-start | bytes 196616 | tf_op jit(solution)/shard_map/ppermute | solution.py:15
  104.3 4.3 %collective-permute-start.19 = (f32[128,128]{0,1:T(8,128)S(1)}, f32[128,128]{0,1:T(8,128)S(1)}, u32[]{:S(2)}, u32[]{:S(2)}) collective-permute-start(f32[128,128]{0,1:T(8,128)S(1)} %convolution_bitcast_fusion.33), channel_id=1, source_target_pairs={{0,2},{1,3},{2,0},{3,1},{4,6},{5,7},{6,4},{7,5},{8,10},{9,11},{10,... | collective-permute-start | bytes 196616 | tf_op jit(solution)/shard_map/ppermute | solution.py:15
  114.9 4.3 %collective-permute-start.21 = (f32[128,128]{0,1:T(8,128)S(1)}, f32[128,128]{0,1:T(8,128)S(1)}, u32[]{:S(2)}, u32[]{:S(2)}) collective-permute-start(f32[128,128]{0,1:T(8,128)S(1)} %convolution_bitcast_fusion.31), channel_id=1, source_target_pairs={{0,8},{4,12},{8,0},{12,4},{16,24},{20,28},{24,16},{28,20},{1,9},{5... | collective-permute-start | bytes 196616 | tf_op jit(solution)/shard_map/ppermute | solution.py:15
  119.9 12.7 %collective-permute-start.22 = (f32[128,128]{0,1:T(8,128)}, f32[128,128]{0,1:T(8,128)}, u32[]{:S(2)}, u32[]{:S(2)}) collective-permute-start(f32[128,128]{0,1:T(8,128)} %add.488), channel_id=1, source_target_pairs={{0,16},{4,20},{8,24},{12,28},{16,0},{20,4},{24,8},{28,12},{1,17},{... | collective-permute-start | bytes 196616 | tf_op jit(solution)/shard_map/ppermute | solution.py:15
  126.1 15.0 %collective-permute-start.26 = (f32[128,128]{0,1:T(8,128)}, f32[128,128]{0,1:T(8,128)}, u32[]{:S(2)}, u32[]{:S(2)}) collective-permute-start(f32[128,128]{0,1:T(8,128)} %copy-done.65), channel_id=1, source_target_pairs={{0,1},{1,0},{2,3},{3,2},{4,5},{5,4},{6,7},{7,6},{8,9},{9,8},{10,11... | collective-permute-start | bytes 196616 | tf_op jit(solution)/shard_map/ppermute | solution.py:15
  127.8 11.4 %collective-permute-start.25 = (f32[128,128]{0,1:T(8,128)}, f32[128,128]{0,1:T(8,128)S(1)}, u32[]{:S(2)}, u32[]{:S(2)}) collective-permute-start(f32[128,128]{0,1:T(8,128)} %copy-done.70), channel_id=1, source_target_pairs={{0,2},{1,3},{2,0},{3,1},{4,6},{5,7},{6,4},{7,5},{8,10},{9,11},{10,... | collective-permute-start | bytes 196616 | tf_op jit(solution)/shard_map/ppermute | solution.py:15
  129.3 7.9 %collective-permute-start.24 = (f32[128,128]{0,1:T(8,128)}, f32[128,128]{0,1:T(8,128)S(1)}, u32[]{:S(2)}, u32[]{:S(2)}) collective-permute-start(f32[128,128]{0,1:T(8,128)} %copy-done.75), channel_id=1, source_target_pairs={{0,4},{4,0},{8,12},{12,8},{16,20},{20,16},{24,28},{28,24},{1,5},{5... | collective-permute-start | bytes 196616 | tf_op jit(solution)/shard_map/ppermute | solution.py:15
  130.8 4.5 %collective-permute-start.23 = (f32[128,128]{0,1:T(8,128)}, f32[128,128]{0,1:T(8,128)S(1)}, u32[]{:S(2)}, u32[]{:S(2)}) collective-permute-start(f32[128,128]{0,1:T(8,128)} %copy-done.80), channel_id=1, source_target_pairs={{0,8},{4,12},{8,0},{12,4},{16,24},{20,28},{24,16},{28,20},{1,9},{5... | collective-permute-start | bytes 196616 | tf_op jit(solution)/shard_map/ppermute | solution.py:15
  153.8 4.3 %collective-permute-start.28 = (f32[128,128]{0,1:T(8,128)S(1)}, f32[128,128]{0,1:T(8,128)S(1)}, u32[]{:S(2)}, u32[]{:S(2)}) collective-permute-start(f32[128,128]{0,1:T(8,128)S(1)} %convolution_bitcast_fusion.29), channel_id=1, source_target_pairs={{0,2},{1,3},{2,0},{3,1},{4,6},{5,7},{6,4},{7,5},{8,10},{9,11},{10,... | collective-permute-start | bytes 196616 | tf_op jit(solution)/shard_map/ppermute | solution.py:15
  168.3 8.0 %collective-permute-start.31 = (f32[128,128]{0,1:T(8,128)}, f32[128,128]{0,1:T(8,128)}, u32[]{:S(2)}, u32[]{:S(2)}) collective-permute-start(f32[128,128]{0,1:T(8,128)} %add.507), channel_id=1, source_target_pairs={{0,16},{4,20},{8,24},{12,28},{16,0},{20,4},{24,8},{28,12},{1,17},{... | collective-permute-start | bytes 196616 | tf_op jit(solution)/shard_map/ppermute | solution.py:15
  172.0 9.2 %collective-permute-start.35 = (f32[128,128]{0,1:T(8,128)}, f32[128,128]{0,1:T(8,128)}, u32[]{:S(2)}, u32[]{:S(2)}) collective-permute-start(f32[128,128]{0,1:T(8,128)} %copy-done.64), channel_id=1, source_target_pairs={{0,1},{1,0},{2,3},{3,2},{4,5},{5,4},{6,7},{7,6},{8,9},{9,8},{10,11... | collective-permute-start | bytes 196616 | tf_op jit(solution)/shard_map/ppermute | solution.py:15
  173.7 6.3 %collective-permute-start.34 = (f32[128,128]{0,1:T(8,128)}, f32[128,128]{0,1:T(8,128)S(1)}, u32[]{:S(2)}, u32[]{:S(2)}) collective-permute-start(f32[128,128]{0,1:T(8,128)} %copy-done.69), channel_id=1, source_target_pairs={{0,2},{1,3},{2,0},{3,1},{4,6},{5,7},{6,4},{7,5},{8,10},{9,11},{10,... | collective-permute-start | bytes 196616 | tf_op jit(solution)/shard_map/ppermute | solution.py:15
  174.2 5.4 %collective-permute-start.33 = (f32[128,128]{0,1:T(8,128)}, f32[128,128]{0,1:T(8,128)S(1)}, u32[]{:S(2)}, u32[]{:S(2)}) collective-permute-start(f32[128,128]{0,1:T(8,128)} %copy-done.74), channel_id=1, source_target_pairs={{0,4},{4,0},{8,12},{12,8},{16,20},{20,16},{24,28},{28,24},{1,5},{5... | collective-permute-start | bytes 196616 | tf_op jit(solution)/shard_map/ppermute | solution.py:15
  174.6 4.5 %collective-permute-start.32 = (f32[128,128]{0,1:T(8,128)}, f32[128,128]{0,1:T(8,128)S(1)}, u32[]{:S(2)}, u32[]{:S(2)}) collective-permute-start(f32[128,128]{0,1:T(8,128)} %copy-done.79), channel_id=1, source_target_pairs={{0,8},{4,12},{8,0},{12,4},{16,24},{20,28},{24,16},{28,20},{1,9},{5... | collective-permute-start | bytes 196616 | tf_op jit(solution)/shard_map/ppermute | solution.py:15
  196.0 4.3 %collective-permute-start.38 = (f32[128,128]{0,1:T(8,128)S(1)}, f32[128,128]{0,1:T(8,128)S(1)}, u32[]{:S(2)}, u32[]{:S(2)}) collective-permute-start(f32[128,128]{0,1:T(8,128)S(1)} %convolution_bitcast_fusion.24), channel_id=1, source_target_pairs={{0,4},{4,0},{8,12},{12,8},{16,20},{20,16},{24,28},{28,24},{1,5},{5... | collective-permute-start | bytes 196616 | tf_op jit(solution)/shard_map/ppermute | solution.py:15
  201.3 4.3 %collective-permute-start.39 = (f32[128,128]{0,1:T(8,128)S(1)}, f32[128,128]{0,1:T(8,128)S(1)}, u32[]{:S(2)}, u32[]{:S(2)}) collective-permute-start(f32[128,128]{0,1:T(8,128)S(1)} %convolution_bitcast_fusion.23), channel_id=1, source_target_pairs={{0,8},{4,12},{8,0},{12,4},{16,24},{20,28},{24,16},{28,20},{1,9},{5... | collective-permute-start | bytes 196616 | tf_op jit(solution)/shard_map/ppermute | solution.py:15
  206.3 12.6 %collective-permute-start.40 = (f32[128,128]{0,1:T(8,128)}, f32[128,128]{0,1:T(8,128)}, u32[]{:S(2)}, u32[]{:S(2)}) collective-permute-start(f32[128,128]{0,1:T(8,128)} %add.526), channel_id=1, source_target_pairs={{0,16},{4,20},{8,24},{12,28},{16,0},{20,4},{24,8},{28,12},{1,17},{... | collective-permute-start | bytes 196616 | tf_op jit(solution)/shard_map/ppermute | solution.py:15
  212.3 15.0 %collective-permute-start.44 = (f32[128,128]{0,1:T(8,128)}, f32[128,128]{0,1:T(8,128)}, u32[]{:S(2)}, u32[]{:S(2)}) collective-permute-start(f32[128,128]{0,1:T(8,128)} %copy-done.66), channel_id=1, source_target_pairs={{0,1},{1,0},{2,3},{3,2},{4,5},{5,4},{6,7},{7,6},{8,9},{9,8},{10,11... | collective-permute-start | bytes 196616 | tf_op jit(solution)/shard_map/ppermute | solution.py:15
  214.0 11.4 %collective-permute-start.43 = (f32[128,128]{0,1:T(8,128)}, f32[128,128]{0,1:T(8,128)S(1)}, u32[]{:S(2)}, u32[]{:S(2)}) collective-permute-start(f32[128,128]{0,1:T(8,128)} %copy-done.71), channel_id=1, source_target_pairs={{0,2},{1,3},{2,0},{3,1},{4,6},{5,7},{6,4},{7,5},{8,10},{9,11},{10,... | collective-permute-start | bytes 196616 | tf_op jit(solution)/shard_map/ppermute | solution.py:15
  215.5 7.9 %collective-permute-start.42 = (f32[128,128]{0,1:T(8,128)}, f32[128,128]{0,1:T(8,128)S(1)}, u32[]{:S(2)}, u32[]{:S(2)}) collective-permute-start(f32[128,128]{0,1:T(8,128)} %copy-done.76), channel_id=1, source_target_pairs={{0,4},{4,0},{8,12},{12,8},{16,20},{20,16},{24,28},{28,24},{1,5},{5... | collective-permute-start | bytes 196616 | tf_op jit(solution)/shard_map/ppermute | solution.py:15
  217.0 4.5 %collective-permute-start.41 = (f32[128,128]{0,1:T(8,128)}, f32[128,128]{0,1:T(8,128)S(1)}, u32[]{:S(2)}, u32[]{:S(2)}) collective-permute-start(f32[128,128]{0,1:T(8,128)} %copy-done.81), channel_id=1, source_target_pairs={{0,8},{4,12},{8,0},{12,4},{16,24},{20,28},{24,16},{28,20},{1,9},{5... | collective-permute-start | bytes 196616 | tf_op jit(solution)/shard_map/ppermute | solution.py:15
  242.5 4.3 %collective-permute-start.46 = (f32[128,128]{0,1:T(8,128)S(1)}, f32[128,128]{0,1:T(8,128)S(1)}, u32[]{:S(2)}, u32[]{:S(2)}) collective-permute-start(f32[128,128]{0,1:T(8,128)S(1)} %convolution_bitcast_fusion.21), channel_id=1, source_target_pairs={{0,2},{1,3},{2,0},{3,1},{4,6},{5,7},{6,4},{7,5},{8,10},{9,11},{10,... | collective-permute-start | bytes 196616 | tf_op jit(solution)/shard_map/ppermute | solution.py:15
  258.1 8.1 %collective-permute-start.49 = (f32[128,128]{0,1:T(8,128)}, f32[128,128]{0,1:T(8,128)}, u32[]{:S(2)}, u32[]{:S(2)}) collective-permute-start(f32[128,128]{0,1:T(8,128)} %add.545), channel_id=1, source_target_pairs={{0,16},{4,20},{8,24},{12,28},{16,0},{20,4},{24,8},{28,12},{1,17},{... | collective-permute-start | bytes 196616 | tf_op jit(solution)/shard_map/ppermute | solution.py:15
  261.8 13.0 %collective-permute-start.53 = (f32[128,128]{0,1:T(8,128)}, f32[128,128]{0,1:T(8,128)}, u32[]{:S(2)}, u32[]{:S(2)}) collective-permute-start(f32[128,128]{0,1:T(8,128)} %copy-done.63), channel_id=1, source_target_pairs={{0,1},{1,0},{2,3},{3,2},{4,5},{5,4},{6,7},{7,6},{8,9},{9,8},{10,11... | collective-permute-start | bytes 196616 | tf_op jit(solution)/shard_map/ppermute | solution.py:15
  263.5 9.4 %collective-permute-start.52 = (f32[128,128]{0,1:T(8,128)}, f32[128,128]{0,1:T(8,128)S(1)}, u32[]{:S(2)}, u32[]{:S(2)}) collective-permute-start(f32[128,128]{0,1:T(8,128)} %copy-done.68), channel_id=1, source_target_pairs={{0,2},{1,3},{2,0},{3,1},{4,6},{5,7},{6,4},{7,5},{8,10},{9,11},{10,... | collective-permute-start | bytes 196616 | tf_op jit(solution)/shard_map/ppermute | solution.py:15
  264.0 6.9 %collective-permute-start.51 = (f32[128,128]{0,1:T(8,128)}, f32[128,128]{0,1:T(8,128)S(1)}, u32[]{:S(2)}, u32[]{:S(2)}) collective-permute-start(f32[128,128]{0,1:T(8,128)} %copy-done.73), channel_id=1, source_target_pairs={{0,4},{4,0},{8,12},{12,8},{16,20},{20,16},{24,28},{28,24},{1,5},{5... | collective-permute-start | bytes 196616 | tf_op jit(solution)/shard_map/ppermute | solution.py:15
  264.5 4.5 %collective-permute-start.50 = (f32[128,128]{0,1:T(8,128)}, f32[128,128]{0,1:T(8,128)S(1)}, u32[]{:S(2)}, u32[]{:S(2)}) collective-permute-start(f32[128,128]{0,1:T(8,128)} %copy-done.78), channel_id=1, source_target_pairs={{0,8},{4,12},{8,0},{12,4},{16,24},{20,28},{24,16},{28,20},{1,9},{5... | collective-permute-start | bytes 196616 | tf_op jit(solution)/shard_map/ppermute | solution.py:15
  286.4 4.3 %collective-permute-start.56 = (f32[128,128]{0,1:T(8,128)S(1)}, f32[128,128]{0,1:T(8,128)S(1)}, u32[]{:S(2)}, u32[]{:S(2)}) collective-permute-start(f32[128,128]{0,1:T(8,128)S(1)} %convolution_bitcast_fusion.16), channel_id=1, source_target_pairs={{0,4},{4,0},{8,12},{12,8},{16,20},{20,16},{24,28},{28,24},{1,5},{5... | collective-permute-start | bytes 196616 | tf_op jit(solution)/shard_map/ppermute | solution.py:15
  288.1 57.9 %collective-permute-start.62 = (f32[128,128]{0,1:T(8,128)S(1)}, f32[128,128]{0,1:T(8,128)S(1)}, u32[]{:S(2)}, u32[]{:S(2)}) collective-permute-start(f32[128,128]{0,1:T(8,128)S(1)} %fusion.95), channel_id=1, source_target_pairs={{0,1},{1,0},{2,3},{3,2},{4,5},{5,4},{6,7},{7,6},{8,9},{9,8},{10,11... | collective-permute-start | bytes 196616 | tf_op jit(solution)/shard_map/ppermute | solution.py:15
  291.0 44.4 %collective-permute-start.57 = (f32[128,128]{0,1:T(8,128)S(1)}, f32[128,128]{0,1:T(8,128)S(1)}, u32[]{:S(2)}, u32[]{:S(2)}) collective-permute-start(f32[128,128]{0,1:T(8,128)S(1)} %convolution_bitcast_fusion.15), channel_id=1, source_target_pairs={{0,8},{4,12},{8,0},{12,4},{16,24},{20,28},{24,16},{28,20},{1,9},{5... | collective-permute-start | bytes 196616 | tf_op jit(solution)/shard_map/ppermute | solution.py:15
  335.4 6.3 %collective-permute-start.58 = (f32[128,128]{0,1:T(8,128)S(1)}, f32[128,128]{0,1:T(8,128)S(1)}, u32[]{:S(2)}, u32[]{:S(2)}) collective-permute-start(f32[128,128]{0,1:T(8,128)S(1)} %add.564), channel_id=1, source_target_pairs={{0,16},{4,20},{8,24},{12,28},{16,0},{20,4},{24,8},{28,12},{1,17},{... | collective-permute-start | bytes 196616 | tf_op jit(solution)/shard_map/ppermute | solution.py:15
  336.8 7.9 %collective-permute-start.61 = (f32[128,128]{0,1:T(8,128)S(1)}, f32[128,128]{0,1:T(8,128)S(1)}, u32[]{:S(2)}, u32[]{:S(2)}) collective-permute-start(f32[128,128]{0,1:T(8,128)S(1)} %add.561), channel_id=1, source_target_pairs={{0,2},{1,3},{2,0},{3,1},{4,6},{5,7},{6,4},{7,5},{8,10},{9,11},{10,... | collective-permute-start | bytes 196616 | tf_op jit(solution)/shard_map/ppermute | solution.py:15
  339.1 5.2 %collective-permute-start.60 = (f32[128,128]{0,1:T(8,128)S(1)}, f32[128,128]{0,1:T(8,128)S(1)}, u32[]{:S(2)}, u32[]{:S(2)}) collective-permute-start(f32[128,128]{0,1:T(8,128)S(1)} %add.562), channel_id=1, source_target_pairs={{0,4},{4,0},{8,12},{12,8},{16,20},{20,16},{24,28},{28,24},{1,5},{5... | collective-permute-start | bytes 196616 | tf_op jit(solution)/shard_map/ppermute | solution.py:15
  (98 other events, 824.9 us)
where the time goes:
time: 356 us; the launch traced here: 351 us
  matrix products  120 us (34%)
  starting transfers between devices  69.2 us (19%)
  waiting for transfers between devices  65.8 us (18%)
  local copies, waits for them, and re-layouts  46.1 us (13%)
  blocking collectives  40.9 us (11%)
  other arithmetic  6.28 us (2%)
    ppermute x63, starting transfers between devices, swapped(): return lax.ppermute(value, axis, pairs)  69.2 us
    ppermute x63, waiting for transfers between devices, swapped(): return lax.ppermute(value, axis, pairs)  65.8 us
    psum x1, blocking collectives, body(): norm_list.append(lax.psum(partial_norm, ('rows', 'leaf')))  40.9 us
    dot_general x28, matrix products, apply_device(): jnp.dot(factor_table[2], sibling_list[height], precision=HIGHEST)  20.8 us
    dot_general x28, matrix products, apply_device(): jnp.dot(factor_table[1], far_field, precision=HIGHEST)  20.6 us
    dot_general x28, matrix products, apply_device(): jnp.dot(cross_tables[height][0].T, coefficient, precision=HIGHEST)  20.3 us
    dot_general x10, matrix products, apply_device(): jnp.einsum('lij,ljc->lic', near_set, piece_value, preferred_element_type=...  16.6 us
    unnamed x168, local copies, waits for them, and re-layouts  10.8 us
  transfers between devices with their start and end apart: 63, of which 34 were waited for; matrix products, arithmetic and copies ran while one was open for 23% of the time, Pallas kernels for 0%

commit v1 on v0

v1 whole, which is shorter than its diff:
```python
import functools
import jax
import jax.numpy as jnp
from jax import lax
from jax.experimental import pallas as pl
from jax.experimental.pallas import tpu as pltpu
from jax.sharding import PartitionSpec as P

STEPS = 3
F32 = jnp.float32
BF16 = jnp.bfloat16
NT = (((1,), (1,)), ((), ()))


def dot(a, b):
    return jnp.dot(a, b, preferred_element_type=F32)


def split(v):
    hi = v.astype(BF16)
    lo = (v - hi.astype(F32)).astype(BF16)
    return hi, lo


def wide(v):
    return jnp.concatenate(split(v), axis=1)


def tall(v):
    return jnp.concatenate(split(v), axis=0)


def fold_cols(v):
    n = v.shape[1] // 2
    return v[:, :n] + v[:, n:]


def fold_rows(v):
    n = v.shape[0] // 2
    return v[:n] + v[n:]


def kernel(
    bits_leaf, bits_rows,
    rhs_hbm, near_hbm, bases_hbm, local_hbm, upper_hbm, top_hbm,
    x_ref, norm_ref,
    b_ref, r_ref, near, bases, local, upper, top,
    vt, pt, tt, cb, pre, nrm,
    send_a, send_b, recv_a, recv_b, send_n, recv_n, sib_full, full,
    load_sem, send_sem, recv_sem,
):
    leaves = near.shape[1]
    rank = bases.shape[4]
    levels = bits_leaf + bits_rows
    last = levels - 1
    root = 2 * leaves - 2
    leaf = lax.axis_index("leaf")
    rows = lax.axis_index("rows")
    half = x_ref.shape[2] // 2
    mine = pl.multiple_of(leaf % 2 * half, half)
    other = pl.multiple_of((1 - leaf % 2) * half, half)
    top_pos = rows // 2 ** (bits_rows - 1)

    def partner(level):
        if level < bits_leaf:
            d = 2**level
            flip = leaf + d - 2 * d * (leaf // d % 2)
            return (rows, flip)
        d = 2 ** (level - bits_leaf)
        flip = rows + d - 2 * d * (rows // d % 2)
        return (flip, leaf)

    def load(src, dst, index):
        return pltpu.make_async_copy(src, dst, load_sem.at[index])

    loads = {}
    order = [("rhs", rhs_hbm, b_ref), ("res", rhs_hbm, r_ref)]
    for s in (1, 0):
        order += [
            (("bases", s), bases_hbm.at[s], bases.at[s]),
            (("local", s), local_hbm.at[s], local.at[s]),
            (("upper", s), upper_hbm.at[s, 0], upper.at[s]),
            (("top", s), top_hbm.at[s], top.at[s]),
            (("near", s), near_hbm.at[s], near.at[s]),
        ]
    for index, (name, src, dst) in enumerate(order):
        loads[name] = load(src, dst, index)
        loads[name].start()

    barrier = pltpu.get_barrier_semaphore()
    for level in range(levels):
        pl.semaphore_signal(
            barrier, inc=1, device_id=partner(level), device_id_type=pl.DeviceIdType.MESH
        )

    def setup_up(s):
        loads["bases", s].wait()
        loads["local", s].wait()
        for i in range(leaves):
            vt[s, i] = bases[s, i, 1].astype(F32).T.astype(BF16)
        for p in range(leaves - 1):
            pair = [local[s, 2 * p + j, 0].astype(F32).T.astype(BF16) for j in range(2)]
            pt[s, p] = jnp.concatenate(pair, axis=1)

    def setup_down(s):
        loads["upper", s].wait()
        loads["top", s].wait()
        chain = None
        for level in range(1, levels):
            coupling = top[s, top_pos] if level == last else upper[s, level - 1, 2]
            if chain is None:
                product = coupling.astype(F32)
            else:
                product = fold_rows(dot(tall(chain), coupling))
            tt[s, level] = wide(product.T)
            if level < last:
                q = upper[s, level - 1, 1]
                chain = q.astype(F32) if chain is None else fold_rows(dot(tall(chain), q))

    def remote(s, index, src, dst, level):
        return pltpu.make_async_remote_copy(
            src_ref=src,
            dst_ref=dst,
            send_sem=send_sem.at[s, index],
            recv_sem=recv_sem.at[s, index],
            device_id=partner(level),
            device_id_type=pl.DeviceIdType.MESH,
        )

    def apply(s, norms, hooks):
        def pieces(i):
            return wide(x_ref[i]) if s == 0 else r_ref[i].astype(BF16)

        def fold(v):
            return fold_cols(v) if s == 0 else v

        def near_leaf(i):
            value = fold(dot(near[s, i], pieces(i)))
            if s == 0:
                r_ref[i] = b_ref[i] - value
            else:
                x_ref[i] = x_ref[i] + value

        def couple(n):
            sibling = n + 1 - 2 * (n % 2)
            pre[n] = fold_cols(dot(local[s, n, 2], cb[sibling]))

        for i in range(leaves):
            cb[i] = wide(fold(dot(vt[s, i], pieces(i))))
        for p in range(leaves - 1):
            stacked = jnp.concatenate([cb[2 * p], cb[2 * p + 1]], axis=0)
            coefficient = fold_cols(dot(pt[s, p], stacked))
            if p < leaves - 2:
                cb[leaves + p] = wide(coefficient)
        started = []

        def start(index, src, dst, level):
            copy = remote(s, index, src, dst, level)
            copy.start()
            started.append(copy)
            return copy

        full[s] = fold_rows(dot(tall(coefficient.T), local[s, root, 0]))
        sib_full[s, 0] = coefficient
        work = list(range(leaves))
        hooks = list(hooks)
        total = nrm[0] if norms is not None else None
        far = None
        previous_b = None
        for level in range(levels):
            base = 3 * level
            if level == 0:
                copy_a = start(base, full.at[s, pl.ds(other, half)], recv_a.at[s, 0], 0)
            else:
                if level == last:
                    send_a[s, level] = value
                else:
                    send_a[s, level] = fold_rows(dot(tall(value), upper[s, level - 1, 0]))
                copy_a = start(base, send_a.at[s, level], recv_a.at[s, level], level)
            if norms is not None:
                send_n[level] = total
                copy_n = start(base + 1, send_n.at[level], recv_n.at[level], level)
            copy_b = None
            if level == 0:
                copy_b = start(base + 2, sib_full.at[s, 0], sib_full.at[s, 1], 0)
            elif level < last:
                send_b[s, level] = value
                copy_b = start(base + 2, send_b.at[s, level], recv_b.at[s, level], level)
            if hooks:
                hooks.pop(0)()
            if work:
                near_leaf(work.pop(0))
            if level == last:
                while work:
                    near_leaf(work.pop(0))
                while hooks:
                    hooks.pop(0)()
            if level == 1:
                for n in range(root):
                    couple(n)
            if previous_b is not None:
                previous_b.wait_recv()
                if level == 1:
                    root_pre = fold_cols(dot(local[s, root, 2], wide(sib_full[s, 1])))
                else:
                    term = across(s, recv_b[s, level - 1], level - 1)
                    far = term if far is None else far + term
            previous_b = copy_b
            copy_a.wait_recv()
            if level == 0:
                value = full[s, pl.ds(mine, half)] + recv_a[s, 0]
            elif level < last:
                value = send_a[s, level] + recv_a[s, level]
            if norms is not None:
                copy_n.wait_recv()
                total = total + recv_n[level]
        term = across(s, recv_a[s, last], last)
        far = term if far is None else far + term
        sib_full[s, 2, pl.ds(mine, half)] = far
        copy = start(
            3 * levels,
            sib_full.at[s, 2, pl.ds(mine, half)],
            sib_full.at[s, 2, pl.ds(mine, half)],
            0,
        )
        if norms is not None:
            nrm[norms] = total
        copy.wait_recv()
        far_t = tall(sib_full[s, 2])
        field = {}
        field[root] = (
            fold_cols(
                lax.dot_general(local[s, root, 1], far_t, NT, preferred_element_type=F32)
            )
            + root_pre
        )
        for n in range(root - 1, -1, -1):
            parent = leaves + n // 2
            if not isinstance(field[parent], tuple):
                field[parent] = (wide(field[parent]),)
            field[n] = fold_cols(dot(local[s, n, 1], field[parent][0])) + pre[n]
        partial = None
        for i in range(leaves):
            if s == 0:
                out = r_ref[i] - fold_cols(dot(bases[s, i, 0], wide(field[i])))
                r_ref[i] = out
                square = jnp.sum((out * out).reshape(-1, 8, out.shape[1]), axis=0)
                partial = square if partial is None else partial + square
            else:
                x_ref[i] = x_ref[i] + dot(bases[s, i, 0], field[i].astype(BF16))
        if s == 0:
            nrm[0] = partial
        for copy in started:
            copy.wait_send()

    def across(s, value, level):
        out = dot(tall(value), tt[s, level])
        n, m = out.shape[0] // 2, out.shape[1] // 2
        return out[:n, :m] + (out[:n, m:] + out[n:, :m])

    setup_up(1)
    x_ref[...] = jnp.zeros(x_ref.shape, F32)
    loads["rhs"].wait()
    loads["res"].wait()
    pl.semaphore_wait(barrier, levels)

    def first():
        setup_down(1)
        loads["near", 1].wait()

    def second():
        setup_up(0)

    def third():
        setup_down(0)
        loads["near", 0].wait()

    apply(1, None, [first, second, third])

    def step(k, carry):
        apply(0, None, [])
        apply(1, k + 1, [])
        return carry

    lax.fori_loop(0, STEPS, step, 0)
    for k in range(STEPS):
        norm_ref[pl.ds(k, 1)] = jnp.sum(nrm[k + 1], axis=0, keepdims=True)


def body(right_sides, near_blocks, leaf_bases, local_factors, upper_factors, top_couplings):
    bits_leaf = lax.axis_size("leaf").bit_length() - 1
    bits_rows = lax.axis_size("rows").bit_length() - 1
    levels = bits_leaf + bits_rows
    leaves, size = near_blocks.shape[1], near_blocks.shape[2]
    rank = leaf_bases.shape[4]
    columns = right_sides.shape[1]
    half = columns // 2
    nodes = local_factors.shape[1]
    heights = upper_factors.shape[2]
    vmem = pltpu.VMEM
    out, norms = pl.pallas_call(
        functools.partial(kernel, bits_leaf, bits_rows),
        out_shape=(
            jax.ShapeDtypeStruct((leaves, size, columns), F32),
            jax.ShapeDtypeStruct((STEPS, columns), F32),
        ),
        in_specs=[pl.BlockSpec(memory_space=pl.ANY)] * 6,
        out_specs=(pl.BlockSpec(memory_space=vmem), pl.BlockSpec(memory_space=vmem)),
        scratch_shapes=[
            vmem((leaves, size, columns), F32),
            vmem((leaves, size, columns), F32),
            vmem((2, leaves, size, size), BF16),
            vmem((2, leaves, 2, size, rank), BF16),
            vmem((2, nodes, 3, rank, rank), BF16),
            vmem((2, heights, 3, rank, rank), BF16),
            vmem((2, 2, rank, rank), BF16),
            vmem((2, leaves, rank, size), BF16),
            vmem((2, leaves - 1, rank, 2 * rank), BF16),
            vmem((2, levels, rank, 2 * rank), BF16),
            vmem((nodes - 1, rank, 2 * columns), BF16),
            vmem((nodes - 1, rank, columns), F32),
            vmem((STEPS + 1, 8, columns), F32),
            vmem((2, levels, half, rank), F32),
            vmem((2, levels, half, rank), F32),
            vmem((2, levels, half, rank), F32),
            vmem((2, levels, half, rank), F32),
            vmem((levels, 8, columns), F32),
            vmem((levels, 8, columns), F32),
            vmem((2, 3, rank, columns), F32),
            vmem((2, columns, rank), F32),
            pltpu.SemaphoreType.DMA((12,)),
            pltpu.SemaphoreType.DMA((2, 3 * levels + 1)),
            pltpu.SemaphoreType.DMA((2, 3 * levels + 1)),
        ],
        compiler_params=pltpu.CompilerParams(
            collective_id=0, has_side_effects=True, vmem_limit_bytes=48 * 1024 * 1024
        ),
    )(
        right_sides.reshape(leaves, size, columns),
        near_blocks,
        leaf_bases,
        local_factors,
        upper_factors,
        top_couplings,
    )
    return out.reshape(-1, columns), norms


def solution(mesh):
    placed = (
        P(("rows", "leaf"), None),
        P(None, ("rows", "leaf"), None, None),
        P(None, ("rows", "leaf"), None, None, None),
        P(None, ("rows", "leaf"), None, None, None),
        P(None, ("rows", "leaf"), None, None, None, None),
        P(),
    )
    return jax.shard_map(
        body,
        mesh=mesh,
        in_specs=placed,
        out_specs=(P(("rows", "leaf"), None), P()),
        check_vma=False,
    )
```

time: 356 us -> 129 us (0.36); the launches traced: 351 us -> 128 us
  Pallas kernels: 0 us -> 121 us
  matrix products: 120 us -> 0 us
  starting transfers between devices: 69.2 us -> 0 us
  waiting for transfers between devices: 65.8 us -> 0 us
  blocking collectives: 40.9 us -> 0 us
  local copies, waits for them, and re-layouts: 46.1 us -> 6.07 us
  other arithmetic: 6.28 us -> 0 us
    pallas_call x0 -> x1, Pallas kernels: none -> 121 us  [body(): pl.pallas_call(functools.partial(kernel, bits_leaf, bits_rows), out_shape...]
    dot_general x163 -> x0, matrix products: 120 us -> none  [the longest x28 20.8 us: apply_device(): jnp.dot(factor_table[2], sibling_list[height], precision=HIGHEST)]
    ppermute x63 -> x0, starting transfers between devices: 69.2 us -> none  [swapped(): return lax.ppermute(value, axis, pairs)]
    ppermute x63 -> x0, waiting for transfers between devices: 65.8 us -> none  [swapped(): return lax.ppermute(value, axis, pairs)]
    psum x1 -> x0, blocking collectives: 40.9 us -> none  [body(): norm_list.append(lax.psum(partial_norm, ('rows', 'leaf')))]
    reshape x8 -> x0, local copies, waits for them, and re-layouts: 12 us -> none  [the longest x7 9.47 us: sibling_of(): return shaped[:, ::-1].reshape(values.shape)]
    rev x7 -> x0, local copies, waits for them, and re-layouts: 9.08 us -> none  [sibling_of(): return shaped[:, ::-1].reshape(values.shape)]
    slice x6 -> x0, local copies, waits for them, and re-layouts: 8.55 us -> none  [the longest x4 6.73 us: apply_device(): factor_table = factors[offset:offset + node_count]]
  transfers between devices with their start and end apart: 63 -> 0, of which waited for: 34 -> 0; matrix products, arithmetic and copies ran while one was open for 23% -> 0% of each run, Pallas kernels for 0% -> 0%
where the time goes in v1:
time: 129 us; the launch traced here: 128 us
  Pallas kernels  121 us (94%)
  local copies, waits for them, and re-layouts  6.07 us (5%)
    pallas_call x1, Pallas kernels, body(): pl.pallas_call(functools.partial(kernel, bits_leaf, bits_rows), out_shape...  121 us
    unnamed x10, local copies, waits for them, and re-layouts  6.07 us

profile of v1, /device:TPU:0, one launch (start us, length us, event | category | flops | bytes accessed | tf_op | source)
XLA Modules:
  0.0 127.9 jit_solution(11089414567622367564)
XLA Ops:
  0.6 0.0 copy-start
  0.6 1.3 %copy-done = bf16[2,7,3,128,128]{4,3,2,1,0:T(8,128)(2,1)S(1)} copy-done((bf16[2,7,3,128,128]{4,3,2,1,0:T(8,128)(2,1)S(1)}, bf16[2,7,3,128,128]{4,3,2,1,0:T(8,128)(2,1)}, u32[]{:S(2)}) %copy-start) | copy-done | bytes 1376280
  2.0 0.0 copy-start.1
  2.0 1.2 copy-done.1
  3.2 0.0 copy-start.2
  3.2 1.1 copy-done.2
  4.3 0.0 copy-start.3
  4.3 0.9 copy-done.3
  5.2 121.2 %shard_map.77 = (f32[4,512,128]{2,1,0:T(8,128)S(1)}, f32[3,128]{1,0:T(4,128)S(1)}) custom-call(f32[4,512,128]{2,1,0:T(8,128)S(1)} %bitcast.2, bf16[2,4,512,512]{3,2,1,0:T(8,128)(2,1)} %near_hbm.1, bf16[2,4,2,512,128]{4,3,2,1,0:T(8,128)(2,1)} %bases_hbm.1, bf16[2,7,3,128,128]{4,3,2,1,0:T(8,128)(2,1)S(1)} %copy-done, ...), custom_call_target="tpu_custom_call" | custom-call | tf_op jit(solution)/shard_map/pallas_call | solution.py:301
  126.3 1.0 copy.10
  127.3 0.6 copy.11
Async XLA Ops:
  0.6 1.3 %copy-start = (bf16[2,7,3,128,128]{4,3,2,1,0:T(8,128)(2,1)S(1)}, bf16[2,7,3,128,128]{4,3,2,1,0:T(8,128)(2,1)}, u32[]{:S(2)}) copy-start(bf16[2,7,3,128,128]{4,3,2,1,0:T(8,128)(2,1)} %local_hbm.1) | copy-start | bytes 4128772
  2.0 1.2 copy-start.1
  3.2 1.1 copy-start.2
  4.3 0.9 copy-start.3

commit v2 on v1

v2 whole, which is shorter than its diff:
```python
import functools
import jax
import jax.numpy as jnp
from jax import lax
from jax.experimental import pallas as pl
from jax.experimental.pallas import tpu as pltpu
from jax.sharding import PartitionSpec as P

STEPS = 3
F32 = jnp.float32
BF16 = jnp.bfloat16
NT = (((1,), (1,)), ((), ()))


def dot(a, b):
    return jnp.dot(a, b, preferred_element_type=F32)


def split(v):
    hi = v.astype(BF16)
    lo = (v - hi.astype(F32)).astype(BF16)
    return hi, lo


def wide(v):
    return jnp.concatenate(split(v), axis=1)


def tall(v):
    return jnp.concatenate(split(v), axis=0)


def fold_cols(v):
    n = v.shape[1] // 2
    return v[:, :n] + v[:, n:]


def fold_rows(v):
    n = v.shape[0] // 2
    return v[:n] + v[n:]


def combine(out):
    n, m = out.shape[0] // 2, out.shape[1] // 2
    return out[:n, :m] + (out[:n, m:] + out[n:, :m])


def group_bits(levels):
    return min(3, levels - 1)


def kernel(
    bits_leaf, bits_rows,
    rhs_hbm, near_hbm, bases_hbm, local_hbm, upper_hbm, top_hbm,
    x_ref, norm_ref,
    b_ref, r_ref, near, bases, local, upper, top,
    vt, pt, tt, et, jt, cb, pre, nrm,
    w_send, w_recv, high_a, high_b, got_a, got_b, plane,
    send_a, send_b, recv_a, recv_b, sib_full, full,
    load_sem, send_sem, recv_sem,
):
    leaves = near.shape[1]
    levels = bits_leaf + bits_rows
    last = levels - 1
    bits = group_bits(levels)
    group = 2**bits
    root = 2 * leaves - 2
    leaf = lax.axis_index("leaf")
    rows = lax.axis_index("rows")
    columns = x_ref.shape[2]
    half = columns // 2
    cut = columns // group
    mine = pl.multiple_of(leaf % 2 * half, half)
    other = pl.multiple_of((1 - leaf % 2) * half, half)
    top_pos = rows // 2 ** (bits_rows - 1)

    def flipped(value, mask):
        for bit in range(mask.bit_length()):
            d = 2**bit
            if mask & d:
                value = value + d - 2 * d * (value // d % 2)
        return value

    def device(mask):
        leaf_mask = mask % 2**bits_leaf
        return (flipped(rows, mask // 2**bits_leaf), flipped(leaf, leaf_mask))

    def member(place):
        row, column = place
        if bits <= bits_leaf:
            return column % group
        return column + 2**bits_leaf * (row % 2 ** (bits - bits_leaf))

    me = member((rows, leaf))
    my_rows = pl.multiple_of(me * cut, cut)

    def load(src, dst, index):
        return pltpu.make_async_copy(src, dst, load_sem.at[index])

    loads = {}
    order = []
    for s in (1, 0):
        order += [
            (("local", s), local_hbm.at[s], local.at[s]),
            (("upper", s), upper_hbm.at[s, 0], upper.at[s]),
            (("bases", s), bases_hbm.at[s], bases.at[s]),
        ]
        if s == 1:
            order += [("res", rhs_hbm, r_ref)]
        order += [
            (("near", s), near_hbm.at[s], near.at[s]),
            (("top", s), top_hbm.at[s], top.at[s]),
        ]
        if s == 1:
            order += [("rhs", rhs_hbm, b_ref)]
    for index, (name, src, dst) in enumerate(order):
        loads[name] = load(src, dst, index)
        loads[name].start()

    barrier = pltpu.get_barrier_semaphore()
    partners = list(range(1, group)) + [2**level for level in range(bits, levels)]
    for mask in partners:
        pl.semaphore_signal(
            barrier, inc=1, device_id=device(mask), device_id_type=pl.DeviceIdType.MESH
        )

    def chain(s, which):
        product = upper[s, bits - 2, which].astype(F32)
        for index in range(bits - 3, -1, -1):
            product = fold_cols(dot(upper[s, index, which], wide(product)))
        node = {root: fold_cols(dot(local[s, root, which], wide(product)))}
        for n in range(root - 1, -1, -1):
            parent = leaves + n // 2
            node[n] = fold_cols(dot(local[s, n, which], wide(node[parent])))
        return [node[i] for i in range(leaves)]

    def setup_chain(s):
        loads["local", s].wait()
        loads["upper", s].wait()
        et[s] = tall(jnp.concatenate([v.T for v in chain(s, 0)], axis=1))

    def setup_up(s):
        loads["bases", s].wait()
        for i in range(leaves):
            vt[s, i] = bases[s, i, 1].astype(F32).T.astype(BF16)

    def setup_pairs(s):
        for p in range(leaves - 1):
            pair = [local[s, 2 * p + j, 0].astype(F32).T.astype(BF16) for j in range(2)]
            pt[s, p] = jnp.concatenate(pair, axis=1)

    def setup_couplings(s):
        loads["top", s].wait()
        for first, stop in ((1, bits), (bits, levels)):
            product = None
            for level in range(first, stop):
                coupling = top[s, top_pos] if level == last else upper[s, level - 1, 2]
                if product is None:
                    value = coupling.astype(F32)
                else:
                    value = fold_rows(dot(tall(product), coupling))
                tt[s, level] = wide(value.T)
                if level + 1 < stop:
                    q = upper[s, level - 1, 1]
                    product = q.astype(F32) if product is None else fold_rows(dot(tall(product), q))

    def setup_down(s):
        jt[s] = tall(jnp.concatenate(chain(s, 1), axis=0))

    def across(s, value, level):
        return combine(dot(tall(value), tt[s, level]))

    def apply(s, norms, hooks):
        started = []
        counter = [0]

        def start(src, dst, mask):
            index = counter[0]
            counter[0] += 1
            copy = pltpu.make_async_remote_copy(
                src_ref=src,
                dst_ref=dst,
                send_sem=send_sem.at[s, index],
                recv_sem=recv_sem.at[s, index],
                device_id=device(mask),
                device_id_type=pl.DeviceIdType.MESH,
            )
            copy.start()
            started.append(copy)
            return copy

        def pieces(i):
            return wide(x_ref[i]) if s == 0 else r_ref[i].astype(BF16)

        def fold(v):
            return fold_cols(v) if s == 0 else v

        def near_leaf(i):
            value = fold(dot(near[s, i], pieces(i)))
            if s == 0:
                r_ref[i] = b_ref[i] - value
            else:
                x_ref[i] = x_ref[i] + value

        def couple(n):
            sibling = n + 1 - 2 * (n % 2)
            pre[n] = fold_cols(dot(local[s, n, 2], cb[sibling]))

        field = {}

        def inner():
            for p in range(leaves - 1):
                stacked = jnp.concatenate([cb[2 * p], cb[2 * p + 1]], axis=0)
                coefficient = fold_cols(dot(pt[s, p], stacked))
                if p < leaves - 2:
                    cb[leaves + p] = wide(coefficient)
            full[s] = fold_rows(dot(tall(coefficient.T), local[s, root, 0]))
            sib_full[s, 0] = coefficient
            copy_a = start(full.at[s, pl.ds(other, half)], recv_a.at[s, 0], 1)
            copies_b = [start(sib_full.at[s, 0], sib_full.at[s, 1], 1)]
            yield
            for level in range(1, bits):
                copy_a.wait_recv()
                if level == 1:
                    value = full[s, pl.ds(mine, half)] + recv_a[s, 0]
                else:
                    value = send_a[s, level - 1] + recv_a[s, level - 1]
                if level < bits - 1:
                    send_a[s, level] = fold_rows(dot(tall(value), upper[s, level - 1, 0]))
                    copy_a = start(send_a.at[s, level], recv_a.at[s, level], 2**level)
                send_b[s, level] = value
                copies_b.append(start(send_b.at[s, level], recv_b.at[s, level], 2**level))
                if level == 1:
                    for n in range(root):
                        couple(n)
                    copies_b[0].wait_recv()
                    root_pre = fold_cols(dot(local[s, root, 2], wide(sib_full[s, 1])))
                yield
            far = None
            for level in range(1, bits):
                copies_b[level].wait_recv()
                term = across(s, recv_b[s, level], level)
                far = term if far is None else far + term
            sib_full[s, 2, pl.ds(mine, half)] = far
            copy = start(
                sib_full.at[s, 2, pl.ds(mine, half)], sib_full.at[s, 2, pl.ds(mine, half)], 1
            )
            yield
            copy.wait_recv()
            far_t = tall(sib_full[s, 2])
            product = lax.dot_general(local[s, root, 1], far_t, NT, preferred_element_type=F32)
            field[root] = fold_cols(product) + root_pre
            for n in range(root - 1, -1, -1):
                parent = leaves + n // 2
                field[n] = fold_cols(dot(local[s, n, 1], wide(field[parent]))) + pre[n]
            yield

        for i in range(leaves):
            cb[i] = wide(fold(dot(vt[s, i], pieces(i))))
        stacked = jnp.concatenate([cb[i] for i in range(leaves)], axis=0)
        outer_t = combine(dot(et[s], stacked)).T
        size = cut if norms is None else cut + 8
        for j in range(group):
            w_send[s, j, :cut] = outer_t[j * cut : (j + 1) * cut]
            if norms is not None:
                w_send[s, j, cut:] = nrm[0]
        copies_w = []
        for e in range(group - 1, 0, -1):
            copies_w.append(
                start(
                    w_send.at[s, member(device(e)), pl.ds(0, size)],
                    w_recv.at[s, e, pl.ds(0, size)],
                    e,
                )
            )
        steps = inner()
        work = list(range(leaves))
        hooks = list(hooks)

        def fill(everything=False):
            if hooks:
                hooks.pop(0)()
            next(steps, None)
            while work:
                near_leaf(work.pop(0))
                if not everything:
                    break

        fill()
        fill()
        for copy in copies_w:
            copy.wait_recv()
        value = w_send[s, me, pl.ds(0, size)]
        for e in range(1, group):
            value = value + w_recv[s, e, pl.ds(0, size)]
        far = None
        for level in range(bits, levels):
            coefficient = value[:cut]
            if level == last:
                high_a[s, level, :cut] = coefficient
            else:
                high_a[s, level, :cut] = fold_rows(
                    dot(tall(coefficient), upper[s, level - 1, 0])
                )
            if norms is not None:
                high_a[s, level, cut:] = value[cut:]
            copy_a = start(
                high_a.at[s, level, pl.ds(0, size)], got_a.at[s, level, pl.ds(0, size)], 2**level
            )
            if level < last:
                high_b[s, level] = coefficient
                copy_b = start(high_b.at[s, level], got_b.at[s, level], 2**level)
            fill(level == last)
            if level == last:
                while hooks:
                    hooks.pop(0)()
            copy_a.wait_recv()
            if level == last:
                term = across(s, got_a[s, level, pl.ds(0, cut)], level)
                if norms is not None:
                    nrm[norms] = value[cut:] + got_a[s, level, pl.ds(cut, 8)]
            else:
                value = high_a[s, level, pl.ds(0, size)] + got_a[s, level, pl.ds(0, size)]
                copy_b.wait_recv()
                term = across(s, got_b[s, level], level)
            far = term if far is None else far + term
        plane[s, pl.ds(my_rows, cut)] = far
        copies_f = []
        for e in range(group - 1, 0, -1):
            piece = plane.at[s, pl.ds(my_rows, cut)]
            copies_f.append(start(piece, piece, e))
        for _ in steps:
            pass
        for copy in copies_f:
            copy.wait_recv()
        outer = combine(
            lax.dot_general(jt[s], tall(plane[s]), NT, preferred_element_type=F32)
        )
        rank = plane.shape[2]
        partial = None
        for i in range(leaves):
            total = field[i] + outer[i * rank : (i + 1) * rank]
            if s == 0:
                out = r_ref[i] - fold_cols(dot(bases[s, i, 0], wide(total)))
                r_ref[i] = out
                square = jnp.sum((out * out).reshape(-1, 8, out.shape[1]), axis=0)
                partial = square if partial is None else partial + square
            else:
                x_ref[i] = x_ref[i] + dot(bases[s, i, 0], total.astype(BF16))
        if s == 0:
            nrm[0] = partial
        for copy in started:
            copy.wait_send()

    setup_chain(1)
    setup_up(1)
    x_ref[...] = jnp.zeros(x_ref.shape, F32)
    loads["res"].wait()
    pl.semaphore_wait(barrier, len(partners))

    def first():
        setup_pairs(1)
        loads["near", 1].wait()

    def second():
        setup_couplings(1)
        setup_down(1)

    def third():
        setup_chain(0)
        setup_up(0)
        setup_pairs(0)

    def fourth():
        setup_couplings(0)
        setup_down(0)
        loads["near", 0].wait()
        loads["rhs"].wait()

    apply(1, None, [first, second, third, fourth])

    def step(k, carry):
        apply(0, None, [])
        apply(1, k + 1, [])
        return carry

    lax.fori_loop(0, STEPS, step, 0)
    for k in range(STEPS):
        norm_ref[pl.ds(k, 1)] = jnp.sum(nrm[k + 1], axis=0, keepdims=True)


def body(right_sides, near_blocks, leaf_bases, local_factors, upper_factors, top_couplings):
    bits_leaf = lax.axis_size("leaf").bit_length() - 1
    bits_rows = lax.axis_size("rows").bit_length() - 1
    levels = bits_leaf + bits_rows
    leaves, size = near_blocks.shape[1], near_blocks.shape[2]
    rank = leaf_bases.shape[4]
    columns = right_sides.shape[1]
    half = columns // 2
    bits = group_bits(levels)
    group = 2**bits
    cut = columns // group
    copies = 2 * (group - 1) + 2 * levels
    nodes = local_factors.shape[1]
    heights = upper_factors.shape[2]
    vmem = pltpu.VMEM
    out, norms = pl.pallas_call(
        functools.partial(kernel, bits_leaf, bits_rows),
        out_shape=(
            jax.ShapeDtypeStruct((leaves, size, columns), F32),
            jax.ShapeDtypeStruct((STEPS, columns), F32),
        ),
        in_specs=[pl.BlockSpec(memory_space=pl.ANY)] * 6,
        out_specs=(pl.BlockSpec(memory_space=vmem), pl.BlockSpec(memory_space=vmem)),
        scratch_shapes=[
            vmem((leaves, size, columns), F32),
            vmem((leaves, size, columns), F32),
            vmem((2, leaves, size, size), BF16),
            vmem((2, leaves, 2, size, rank), BF16),
            vmem((2, nodes, 3, rank, rank), BF16),
            vmem((2, heights, 3, rank, rank), BF16),
            vmem((2, 2, rank, rank), BF16),
            vmem((2, leaves, rank, size), BF16),
            vmem((2, leaves - 1, rank, 2 * rank), BF16),
            vmem((2, levels, rank, 2 * rank), BF16),
            vmem((2, 2 * rank, leaves * rank), BF16),
            vmem((2, 2 * leaves * rank, rank), BF16),
            vmem((nodes - 1, rank, 2 * columns), BF16),
            vmem((nodes - 1, rank, columns), F32),
            vmem((STEPS + 1, 8, columns), F32),
            vmem((2, group, cut + 8, rank), F32),
            vmem((2, group, cut + 8, rank), F32),
            vmem((2, levels, cut + 8, rank), F32),
            vmem((2, levels, cut, rank), F32),
            vmem((2, levels, cut + 8, rank), F32),
            vmem((2, levels, cut, rank), F32),
            vmem((2, columns, rank), F32),
            vmem((2, bits, half, rank), F32),
            vmem((2, bits, half, rank), F32),
            vmem((2, bits, half, rank), F32),
            vmem((2, bits, half, rank), F32),
            vmem((2, 3, rank, columns), F32),
            vmem((2, columns, rank), F32),
            pltpu.SemaphoreType.DMA((12,)),
            pltpu.SemaphoreType.DMA((2, copies)),
            pltpu.SemaphoreType.DMA((2, copies)),
        ],
        compiler_params=pltpu.CompilerParams(
            collective_id=0, has_side_effects=True, vmem_limit_bytes=48 * 1024 * 1024
        ),
    )(
        right_sides.reshape(leaves, size, columns),
        near_blocks,
        leaf_bases,
        local_factors,
        upper_factors,
        top_couplings,
    )
    return out.reshape(-1, columns), norms


def solution(mesh):
    placed = (
        P(("rows", "leaf"), None),
        P(None, ("rows", "leaf"), None, None),
        P(None, ("rows", "leaf"), None, None, None),
        P(None, ("rows", "leaf"), None, None, None),
        P(None, ("rows", "leaf"), None, None, None, None),
        P(),
    )
    return jax.shard_map(
        body,
        mesh=mesh,
        in_specs=placed,
        out_specs=(P(("rows", "leaf"), None), P()),
        check_vma=False,
    )
```

time: 129 us -> 112 us (0.87)
  Pallas kernels: 121 us -> 105 us
    pallas_call x1, Pallas kernels: 121 us -> 105 us  [body(): pl.pallas_call(functools.partial(kernel, bits_leaf, bits_rows), out_shape...]
where the time goes in v2:
time: 112 us
  Pallas kernels  105 us (94%)
  local copies, waits for them, and re-layouts  6.07 us (5%)
    pallas_call x1, Pallas kernels, body(): pl.pallas_call(functools.partial(kernel, bits_leaf, bits_rows), out_shape...  105 us
    unnamed x10, local copies, waits for them, and re-layouts  6.07 us

profile of v2, /device:TPU:0, one launch (start us, length us, event | category | flops | bytes accessed | tf_op | source)
XLA Modules:
  0.0 111.7 jit_solution(352857415862927635)
XLA Ops:
  0.6 0.0 copy-start
  0.6 1.3 %copy-done = bf16[2,7,3,128,128]{4,3,2,1,0:T(8,128)(2,1)S(1)} copy-done((bf16[2,7,3,128,128]{4,3,2,1,0:T(8,128)(2,1)S(1)}, bf16[2,7,3,128,128]{4,3,2,1,0:T(8,128)(2,1)}, u32[]{:S(2)}) %copy-start) | copy-done | bytes 1376280
  2.0 0.0 copy-start.1
  2.0 1.2 %copy-done.1 = f32[2048,128]{1,0:T(8,128)S(1)} copy-done((f32[2048,128]{1,0:T(8,128)S(1)}, f32[2048,128]{1,0:T(8,128)}, u32[]{:S(2)}) %copy-start.1) | copy-done | bytes 1048600
  3.2 0.0 copy-start.2
  3.2 1.1 copy-done.2
  4.3 0.0 copy-start.3
  4.3 0.9 copy-done.3
  5.2 104.9 %shard_map.77 = (f32[4,512,128]{2,1,0:T(8,128)S(1)}, f32[3,128]{1,0:T(4,128)S(1)}) custom-call(f32[4,512,128]{2,1,0:T(8,128)S(1)} %bitcast.2, bf16[2,4,512,512]{3,2,1,0:T(8,128)(2,1)} %near_hbm.1, bf16[2,4,2,512,128]{4,3,2,1,0:T(8,128)(2,1)} %bases_hbm.1, bf16[2,7,3,128,128]{4,3,2,1,0:T(8,128)(2,1)S(1)} %copy-done, ...), custom_call_target="tpu_custom_call" | custom-call | tf_op jit(solution)/shard_map/pallas_call | solution.py:407
  110.1 1.0 copy.10
  111.1 0.6 copy.11
Async XLA Ops:
  0.6 1.3 %copy-start = (bf16[2,7,3,128,128]{4,3,2,1,0:T(8,128)(2,1)S(1)}, bf16[2,7,3,128,128]{4,3,2,1,0:T(8,128)(2,1)}, u32[]{:S(2)}) copy-start(bf16[2,7,3,128,128]{4,3,2,1,0:T(8,128)(2,1)} %local_hbm.1) | copy-start | bytes 4128772
  2.0 1.2 %copy-start.1 = (f32[2048,128]{1,0:T(8,128)S(1)}, f32[2048,128]{1,0:T(8,128)}, u32[]{:S(2)}) copy-start(f32[2048,128]{1,0:T(8,128)} %param.6) | copy-start | bytes 3145732
  3.2 1.1 copy-start.2
  4.3 0.9 copy-start.3

commit v3 on v2

--- a/solution.py
+++ b/solution.py
@@ -46,7 +46,7 @@
 
 
 def group_bits(levels):
-    return min(3, levels - 1)
+    return min(3, levels - 2)
 
 
 def kernel(
@@ -119,6 +119,7 @@
 
     barrier = pltpu.get_barrier_semaphore()
     partners = list(range(1, group)) + [2**level for level in range(bits, levels)]
+    partners.append(2**last + 2 ** (last - 1))
     for mask in partners:
         pl.semaphore_signal(
             barrier, inc=1, device_id=device(mask), device_id_type=pl.DeviceIdType.MESH
@@ -294,36 +295,53 @@
         for e in range(1, group):
             value = value + w_recv[s, e, pl.ds(0, size)]
         far = None
-        for level in range(bits, levels):
+        for level in range(bits, last - 1):
             coefficient = value[:cut]
-            if level == last:
-                high_a[s, level, :cut] = coefficient
-            else:
-                high_a[s, level, :cut] = fold_rows(
-                    dot(tall(coefficient), upper[s, level - 1, 0])
-                )
+            high_a[s, level, :cut] = fold_rows(dot(tall(coefficient), upper[s, level - 1, 0]))
             if norms is not None:
                 high_a[s, level, cut:] = value[cut:]
             copy_a = start(
                 high_a.at[s, level, pl.ds(0, size)], got_a.at[s, level, pl.ds(0, size)], 2**level
             )
-            if level < last:
-                high_b[s, level] = coefficient
-                copy_b = start(high_b.at[s, level], got_b.at[s, level], 2**level)
-            fill(level == last)
-            if level == last:
-                while hooks:
-                    hooks.pop(0)()
+            high_b[s, level] = coefficient
+            copy_b = start(high_b.at[s, level], got_b.at[s, level], 2**level)
+            fill()
             copy_a.wait_recv()
-            if level == last:
-                term = across(s, got_a[s, level, pl.ds(0, cut)], level)
-                if norms is not None:
-                    nrm[norms] = value[cut:] + got_a[s, level, pl.ds(cut, 8)]
-            else:
-                value = high_a[s, level, pl.ds(0, size)] + got_a[s, level, pl.ds(0, size)]
-                copy_b.wait_recv()
-                term = across(s, got_b[s, level], level)
+            value = high_a[s, level, pl.ds(0, size)] + got_a[s, level, pl.ds(0, size)]
+            copy_b.wait_recv()
+            term = across(s, got_b[s, level], level)
             far = term if far is None else far + term
+        low, high = last - 1, last
+        coefficient = value[:cut]
+        high_a[s, high, :cut] = fold_rows(dot(tall(coefficient), upper[s, low - 1, 0]))
+        high_a[s, low, :cut] = coefficient
+        if norms is not None:
+            high_a[s, high, cut:] = value[cut:]
+            high_a[s, low, cut:] = value[cut:]
+        copies_top = [
+            start(high_a.at[s, src, pl.ds(0, size)], got_a.at[s, dst, pl.ds(0, size)], mask)
+            for src, dst, mask in (
+                (high, high + 1, 2**high + 2**low),
+                (high, high, 2**high),
+                (low, low, 2**low),
+            )
+        ]
+        fill()
+        copies_top[2].wait_recv()
+        got = got_a[s, low, pl.ds(0, size)]
+        if norms is not None:
+            value = value + got
+        term = across(s, got[:cut], low)
+        far = term if far is None else far + term
+        fill(True)
+        while hooks:
+            hooks.pop(0)()
+        copies_top[1].wait_recv()
+        copies_top[0].wait_recv()
+        got = got_a[s, high, pl.ds(0, size)] + got_a[s, high + 1, pl.ds(0, size)]
+        if norms is not None:
+            nrm[norms] = value[cut:] + got[cut:]
+        far = far + across(s, got[:cut], high)
         plane[s, pl.ds(my_rows, cut)] = far
         copies_f = []
         for e in range(group - 1, 0, -1):
@@ -432,7 +450,7 @@
             vmem((2, group, cut + 8, rank), F32),
             vmem((2, levels, cut + 8, rank), F32),
             vmem((2, levels, cut, rank), F32),
-            vmem((2, levels, cut + 8, rank), F32),
+            vmem((2, levels + 1, cut + 8, rank), F32),
             vmem((2, levels, cut, rank), F32),
             vmem((2, columns, rank), F32),
             vmem((2, bits, half, rank), F32),
@@ -446,7 +464,7 @@
             pltpu.SemaphoreType.DMA((2, copies)),
         ],
         compiler_params=pltpu.CompilerParams(
-            collective_id=0, has_side_effects=True, vmem_limit_bytes=48 * 1024 * 1024
+            collective_id=0, has_side_effects=True, vmem_limit_bytes=67043328
         ),
     )(
         right_sides.reshape(leaves, size, columns),

time: 112 us -> 100 us (0.89)
  Pallas kernels: 105 us -> 96.6 us
  local copies, waits for them, and re-layouts: 6.07 us -> 2.84 us
    pallas_call x1, Pallas kernels: 105 us -> 96.6 us  [body(): pl.pallas_call(functools.partial(kernel, bits_leaf, bits_rows), out_shape...]
    unnamed x10 -> x4, local copies, waits for them, and re-layouts: 6.07 us -> 2.84 us
where the time goes in v3:
time: 100 us
  Pallas kernels  96.6 us (97%)
  local copies, waits for them, and re-layouts  2.84 us (3%)
    pallas_call x1, Pallas kernels, body(): pl.pallas_call(functools.partial(kernel, bits_leaf, bits_rows), out_shape...  96.6 us
    unnamed x4, local copies, waits for them, and re-layouts  2.84 us

profile of v3, /device:TPU:0, one launch (start us, length us, event | category | flops | bytes accessed | tf_op | source)
XLA Modules:
  0.0 100.1 jit_solution(15846794920865278780)
XLA Ops:
  0.6 96.6 %shard_map.77 = (f32[4,512,128]{2,1,0:T(8,128)}, f32[3,128]{1,0:T(4,128)}) custom-call(f32[4,512,128]{2,1,0:T(8,128)} %bitcast.2, bf16[2,4,512,512]{3,2,1,0:T(8,128)(2,1)} %near_hbm.1, bf16[2,4,2,512,128]{4,3,2,1,0:T(8,128)(2,1)} %bases_hbm.1, bf16[2,7,3,128,128]{4,3,2,1,0:T(8,128)(2,1)} %local_hbm.1, bf16[2,1,3,3,128,128]{5,4,3,2,1,0:T(8,128)(2,1)} %upper_hbm.1, ...), custom_call_target="tpu_custom_call" | custom-call | tf_op jit(solution)/shard_map/pallas_call | solution.py:425
  97.3 0.0 copy-start
  97.3 2.3 %copy.10 = f32[2048,128]{1,0:T(8,128)} copy(f32[2048,128]{1,0:T(8,128)} %bitcast.3) | data formatting | bytes 2097152
  99.5 0.0 copy-done
  99.5 0.6 copy.11
Async XLA Ops:
  97.3 2.3 %copy-start = (f32[3,128]{1,0:T(4,128)S(1)}, f32[3,128]{1,0:T(4,128)}, u32[]{:S(2)}) copy-start(f32[3,128]{1,0:T(4,128)} %get-tuple-element.9) | copy-start | bytes 4612
